TPU v7x, 32 devices: a whole 2x2x4 slice. The times are simulated.
32 devices in a mesh: dp: 8 (over z, x), patch: 4 (over y, core).
Axes of the slice: x: 2, y: 2, z: 4, core: 2. Of those that a mesh axis runs over, the one named last changes fastest.
Arguments:
- token_ids: int32 [128], replicated, may hold values from 0 to 31999
- parents: int32 [128], replicated, may hold values from 0 to 3
- embedding: bfloat16 [32000, 1024], P('dp'), may hold values from -6 to 6
- self_gain: bfloat16 [1024], replicated, may hold values from 0.25 to 1.75
- query_weight: bfloat16 [1024, 1024], P(None, 'patch'), may hold values from -0.1875 to 0.1875
- key_weight: bfloat16 [1024, 1024], P(None, 'patch'), may hold values from -0.1875 to 0.1875
- value_weight: bfloat16 [1024, 1024], P(None, 'patch'), may hold values from -0.1875 to 0.1875
- output_weight: bfloat16 [1024, 1024], P('patch'), may hold values from -0.75 to 0.75
- past_keys: bfloat16 [128, 128, 1024], P('dp', None, 'patch'), may hold values from -200 to 200
- past_values: bfloat16 [128, 128, 1024], P('dp', None, 'patch'), may hold values from -6 to 6
- cross_gain: bfloat16 [1024], replicated, may hold values from 0.25 to 1.75
- cross_query: bfloat16 [1024, 1024], replicated, may hold values from -0.1875 to 0.1875
- cross_output: bfloat16 [1024, 1024], replicated, may hold values from -0.75 to 0.75
- image_keys: bfloat16 [8, 16, 256, 1024], P('dp', None, 'patch'), may hold values from -260 to 260
- image_values: bfloat16 [8, 16, 256, 1024], P('dp', None, 'patch'), may hold values from -6 to 6
Outputs:
- hidden: bfloat16 [128, 1024], P('dp')
- new_keys: bfloat16 [128, 1024], P('dp', 'patch')
- new_values: bfloat16 [128, 1024], P('dp', 'patch')
Inputs may be any that keep to these rules, and one draw needn't show every extreme that they name: `parents`: a beam of the row's own image.
All inputs are finite; a program needn't handle non-finite values.
Results may differ from a plain program's by a relative error of at most 0.019.
The roundings to bfloat16 on the way count: a program that leaves them out, or rounds other values in their place, can miss the bound.
Values may be sent and summed in bfloat16 or wider, within the bound.
No kernel may reach another device: no remote copies, remote signals or barrier semaphores. Data moves between devices by JAX's collectives and lax.ppermute only.
A program may use at most 64 MiB of HBM per device.

v0:
```python
import math
import jax
import jax.numpy as jnp
from jax import lax
from jax.sharding import PartitionSpec as P

D = 1024
HEADS = 16
BEAMS = 4


def from_partner(value, axis, distance):
    mask = 2**distance
    pairs = [(source, source ^ mask) for source in range(lax.axis_size(axis))]
    return lax.ppermute(value, axis, pairs)


def joined(x, axis, combine):
    everything = jax.tree.map(lambda part: lax.all_gather(part, axis), x)
    first = jax.tree.map(lambda part: part[0], everything)

    def step(k, so_far):
        return combine(so_far, jax.tree.map(lambda part: part[k], everything))

    return lax.fori_loop(1, lax.axis_size(axis), step, first)


def normalize(inputs, gains):
    factor = lax.rsqrt(jnp.mean(inputs * inputs, axis=-1, keepdims=True) + 1e-06)
    return (inputs * factor * gains.astype(jnp.float32)).astype(jnp.bfloat16)


def combine(former, latter):
    peak_former, total_former, sum_former = former
    peak_latter, total_latter, sum_latter = latter
    peaks = jnp.maximum(peak_former, peak_latter)
    former_scale = jnp.exp(peak_former - peaks)
    latter_scale = jnp.exp(peak_latter - peaks)
    heads_count = peaks.shape[-1]
    count_rows = peaks.shape[0]
    sums = (
        sum_former.reshape(count_rows, heads_count, -1) * former_scale[..., None]
        + sum_latter.reshape(count_rows, heads_count, -1) * latter_scale[..., None]
    )
    return (
        peaks,
        total_former * former_scale + total_latter * latter_scale,
        sums.reshape(count_rows, -1),
    )


def beam_collect(pieces, concat_dim):
    for bit_index in range(2):
        partner = from_partner(pieces, "dp", bit_index)
        upper_bit = lax.axis_index("dp") // 2**bit_index % 2
        pieces = jnp.where(
            upper_bit == 1,
            jnp.concatenate([partner, pieces], concat_dim),
            jnp.concatenate([pieces, partner], concat_dim),
        )
    return pieces


def beam_reduce(partial_value):
    for bit_index in (1, 0):
        upper_bit = lax.axis_index("dp") // 2**bit_index % 2
        half_rows = partial_value[0].shape[0] // 2
        keep_part = tuple(
            (
                lax.dynamic_slice_in_dim(member, upper_bit * half_rows, half_rows, 0)
                for member in partial_value
            )
        )
        send_part = tuple(
            (
                lax.dynamic_slice_in_dim(member, (1 - upper_bit) * half_rows, half_rows, 0)
                for member in partial_value
            )
        )
        received = from_partner(send_part, "dp", bit_index)
        partial_value = combine(keep_part, received)
    return partial_value


def patch_merge(partial_value):
    return joined(partial_value, "patch", combine)


def shards(
    token_ids,
    parents,
    embedding,
    self_gain,
    query_weight,
    key_weight,
    value_weight,
    output_weight,
    past_keys,
    past_values,
    cross_gain,
    cross_query,
    cross_output,
    image_keys,
    image_values,
):
    row_count = past_keys.shape[0]
    length = past_keys.shape[1]
    width_here = query_weight.shape[1]
    head_size = D // HEADS
    heads_here = width_here // head_size
    scaling = 1.0 / math.sqrt(head_size)
    position = lax.axis_index("dp")
    slab = embedding.shape[0]
    vocab_ids = position * slab + jnp.arange(slab, dtype=jnp.int32)
    onehot_table = (token_ids[:, None] == vocab_ids[None, :]).astype(jnp.bfloat16)
    tokens = lax.psum_scatter(
        jnp.dot(onehot_table, embedding, preferred_element_type=jnp.float32),
        "dp",
        scatter_dimension=0,
        tiled=True,
    )
    normed = normalize(tokens, self_gain)
    queries = jnp.dot(normed, query_weight, preferred_element_type=jnp.float32).astype(jnp.bfloat16)
    new_key = jnp.dot(normed, key_weight, preferred_element_type=jnp.float32).astype(jnp.bfloat16)
    new_value = jnp.dot(normed, value_weight, preferred_element_type=jnp.float32).astype(
        jnp.bfloat16
    )
    query_heads = queries.reshape(row_count, heads_here, head_size)
    key_heads = new_key.reshape(row_count, heads_here, head_size)
    value_heads = new_value.reshape(row_count, heads_here, head_size)
    own_score = (
        jnp.sum(query_heads.astype(jnp.float32) * key_heads.astype(jnp.float32), axis=-1) * scaling
    )
    paired = jnp.stack([queries, new_key], 0)
    gathered = beam_collect(paired, 1).reshape(2, BEAMS, row_count, heads_here, head_size)
    gathered_queries = gathered[0]
    gathered_keys = gathered[1]
    own_every = (
        jnp.sum(gathered_queries.astype(jnp.float32) * gathered_keys.astype(jnp.float32), axis=-1)
        * scaling
    )
    block_start = position // BEAMS * BEAMS * row_count
    block_parents = lax.dynamic_slice_in_dim(parents, block_start, BEAMS * row_count, 0).reshape(
        BEAMS, row_count
    )
    living = (block_parents == position % BEAMS).astype(jnp.float32)
    old_keys = past_keys.reshape(row_count, length, heads_here, head_size)
    old_values = past_values.reshape(row_count, length, heads_here, head_size)
    scores = (
        jnp.einsum(
            "bihe,ilhe->bihl", gathered_queries, old_keys, preferred_element_type=jnp.float32
        )
        * scaling
    )
    maxima = jnp.maximum(jnp.max(scores, axis=-1), own_every)
    powers = jnp.exp(scores - maxima[..., None]) * living[:, :, None, None]
    totals = jnp.sum(powers, axis=-1) + jnp.exp(own_every - maxima) * living[:, :, None]
    numerators = jnp.einsum(
        "bihl,ilhe->bihe",
        powers.astype(jnp.bfloat16),
        old_values,
        preferred_element_type=jnp.float32,
    )
    partial_value = (
        jnp.where(living[:, :, None] > 0.5, maxima, -1e30).reshape(BEAMS * row_count, heads_here),
        totals.reshape(BEAMS * row_count, heads_here),
        numerators.reshape(BEAMS * row_count, width_here),
    )
    peaks, sums, weighted = beam_reduce(partial_value)
    own_weight = jnp.exp(own_score - peaks).astype(jnp.bfloat16).astype(jnp.float32)
    weighted = weighted.reshape(row_count, heads_here, head_size) + own_weight[
        ..., None
    ] * value_heads.astype(jnp.float32)
    self_context = weighted / sums[..., None]
    self_context = self_context.reshape(row_count, width_here).astype(jnp.bfloat16)
    middle = tokens + lax.psum(
        jnp.dot(self_context, output_weight, preferred_element_type=jnp.float32), "patch"
    )
    probes = jnp.dot(
        normalize(middle, cross_gain), cross_query, preferred_element_type=jnp.float32
    ).astype(jnp.bfloat16)
    every_probe = beam_collect(probes, 0).reshape(BEAMS, row_count, HEADS, head_size)
    patch_count = image_keys.shape[2]
    patch_keys = image_keys.reshape(row_count, patch_count, HEADS, head_size)
    patch_values = image_values.reshape(row_count, patch_count, HEADS, head_size)
    cross_scores = (
        jnp.einsum("bihe,iphe->bihp", every_probe, patch_keys, preferred_element_type=jnp.float32)
        * scaling
    )
    cross_peaks = jnp.max(cross_scores, axis=-1)
    cross_powers = jnp.exp(cross_scores - cross_peaks[..., None])
    cross_totals = jnp.sum(cross_powers, axis=-1)
    cross_sums = jnp.einsum(
        "bihp,iphe->bihe",
        cross_powers.astype(jnp.bfloat16),
        patch_values,
        preferred_element_type=jnp.float32,
    )
    partial_value = (
        cross_peaks.reshape(BEAMS * row_count, HEADS),
        cross_totals.reshape(BEAMS * row_count, HEADS),
        cross_sums.reshape(BEAMS * row_count, D),
    )
    partial_value = beam_reduce(patch_merge(partial_value))
    cross_context = (
        (partial_value[2].reshape(row_count, HEADS, head_size) / partial_value[1][..., None])
        .reshape(row_count, D)
        .astype(jnp.bfloat16)
    )
    hidden = (
        middle + jnp.dot(cross_context, cross_output, preferred_element_type=jnp.float32)
    ).astype(jnp.bfloat16)
    return (hidden, new_key, new_value)


def solution(mesh):
    in_specs = (
        P(),
        P(),
        P("dp", None),
        P(),
        P(None, "patch"),
        P(None, "patch"),
        P(None, "patch"),
        P("patch", None),
        P("dp", None, "patch"),
        P("dp", None, "patch"),
        P(),
        P(),
        P(),
        P("dp", None, "patch", None),
        P("dp", None, "patch", None),
    )
    out_specs = (P("dp", None), P("dp", "patch"), P("dp", "patch"))
    return jax.shard_map(shards, mesh=mesh, in_specs=in_specs, out_specs=out_specs, check_vma=False)
```

profile of v0, /device:TPU:0, one launch (start us, length us, event | category | flops | bytes accessed | tf_op | source)
XLA Modules:
  0.0 208.8 jit_solution(12373102557429961516)
XLA Ops:
  7.3 5.6 %fusion.7 = f32[128,1024]{1,0:T(8,128)} fusion(bf16[4000,1024]{1,0:T(8,128)(2,1)} %param.19, s32[4000]{0:T(1024)S(1)} %iota_add_fusion, s32[128]{0:T(128)} %param.17), kind=kOutput, calls=%fused_computation.12 | convolution fusion | flops 1049088000 | bytes 8732800 | tf_op jit(solution)/shard_map/dot_general | solution.py:117
  13.0 65.4 %reduce-scatter.2.cloned.1.call-done = f32[16,1024]{1,0:T(8,128)} async-done(((f32[128,1024]{1,0:T(8,128)}), f32[16,1024]{1,0:T(8,128)}) %reduce-scatter.2.cloned.1.call-update) | async-done | bytes 65552 | tf_op jit(solution)/shard_map/reduce_scatter | solution.py:116
  80.7 1.4 collective-permute-start
  82.1 1.6 copy.108
  83.9 2.3 %copy.114 = bf16[16,128,256]{1,2,0:T(8,128)(2,1)} copy(bf16[16,128,256]{2,1,0:T(8,128)(2,1)} %param.26) | data formatting | bytes 2097152 | tf_op args[9]
  86.2 1.6 collective-permute-start.1
  87.8 1.2 convolution_convert_fusion.1
  91.9 1.9 convolution_bitcast_fusion
  94.5 1.6 collective-permute-start.2
  96.5 1.5 collective-permute-start.3
  98.3 1.6 collective-permute-done.6
  100.8 1.5 collective-permute-start.7
  107.3 29.6 %all-reduce.2.cloned.1.call-done = f32[16,1024]{1,0:T(8,128)} async-done(((f32[16,1024]{1,0:T(8,128)}), f32[16,1024]{1,0:T(8,128)}) %all-reduce.2.cloned.1.call-update) | async-done | bytes 65552 | tf_op jit(solution)/shard_map/psum | solution.py:176
  138.3 1.5 collective-permute-start.8
  139.8 2.4 %collective-permute-done.8 = bf16[16,1024]{1,0:T(8,128)(2,1)S(1)} collective-permute-done((bf16[16,1024]{1,0:T(8,128)(2,1)S(1)}, bf16[16,1024]{1,0:T(8,128)(2,1)S(1)}, u32[]{:S(2)}, u32[]{:S(2)}) %collective-permute-start.8) | collective-permute-done | bytes 32800 | tf_op jit(solution)/shard_map/ppermute | solution.py:15
  142.2 1.6 collective-permute-start.9
  143.8 6.4 %reshape.165 = bf16[16,64,16,64]{3,2,1,0:T(8,128)(2,1)} reshape(bf16[1,16,64,1024]{3,2,1,0:T(8,128)(2,1)} %param.30) | data formatting | bytes 4194304 | tf_op jit(solution)/shard_map/reshape | solution.py:184
  150.1 6.4 %reshape.166 = bf16[16,64,16,64]{3,2,1,0:T(8,128)(2,1)} reshape(bf16[1,16,64,1024]{3,2,1,0:T(8,128)(2,1)} %param.31) | data formatting | bytes 4194304 | tf_op jit(solution)/shard_map/reshape | solution.py:185
  156.8 4.7 %fusion.51 = (f32[4,16,16]{0,2,1:T(8,128)S(1)}, f32[4,16,16,64]{3,0,2,1:T(4,128)S(1)}) fusion(bf16[16,64,16,64]{3,2,1,0:T(8,128)(2,1)} %reshape.165, bf16[4,16,16,64]{3,2,1,0:T(8,128)(2,1)S(1)} %select_n.148), kind=kOutput, calls=%fused_computation.109 | convolution fusion | flops 8518656 | bytes 2494464 | tf_op jit(solution)/shard_map/bihe,iphe->bihp/dot_general | solution.py:187
  161.5 1.3 fusion.9
  164.9 5.2 %all_gather.10 = f32[4,64,16]{1,2,0:T(8,128)S(1)} all-gather(f32[1,64,16]{1,2,0:T(8,128)S(1)} %all_gather_reshape.10), channel_id=1, replica_groups=mesh['dp'=8,'patch'=4] {'patch'}, dimensions={0}, use_global_device_ids=true | all-gather | bytes 20480 | tf_op jit(solution)/shard_map/all_gather | solution.py:19
  170.1 5.4 %all_gather.9 = f32[4,64,16]{1,2,0:T(8,128)S(1)} all-gather(f32[1,64,16]{1,2,0:T(8,128)S(1)} %all_gather_reshape.9), channel_id=1, replica_groups=mesh['dp'=8,'patch'=4] {'patch'}, dimensions={0}, use_global_device_ids=true | all-gather | bytes 20480 | tf_op jit(solution)/shard_map/all_gather | solution.py:19
  175.5 4.3 %all-gather.2.cloned.1.call-done = f32[4,64,1024]{2,1,0:T(8,128)} async-done(((f32[1,64,1024]{2,1,0:T(8,128)}), f32[4,64,1024]{2,1,0:T(8,128)}) %all-gather.2.cloned.1.call-update) | async-done | bytes 1048592 | tf_op jit(solution)/shard_map/all_gather | solution.py:19
  180.8 6.1 %while.19 = (s32[]{:T(128)}, f32[64,16]{0,1:T(8,128)S(1)}, f32[64,16]{0,1:T(8,128)S(1)}, f32[64,1024]{1,0:T(8,128)S(1)}, f32[4,64,16]{1,2,0:T(8,128)S(1)}, /*ind...) while((s32[]{:T(128)}, f32[64,16]{0,1:T(8,128)S(1)}, ...), condition=%wide.region_11.12_spmd, body=%wide.region_10.11_spmd.sunk | while | flops 202757 | bytes 2941079 | solution.py:25
  185.8 1.1 fusion.67
  187.0 1.5 collective-permute-start.10
  189.1 1.6 collective-permute-start.11
  190.7 1.6 collective-permute-done.14
  193.1 1.5 collective-permute-start.12
  195.4 1.5 collective-permute-start.13
  196.9 1.5 collective-permute-done.15
  199.7 2.6 %fusion.19 = bf16[16,1024]{1,0:T(8,128)(2,1)} fusion(f32[16,1024]{1,0:T(8,128)S(1)} %get-tuple-element.210, bf16[1024,1024]{1,0:T(8,128)(2,1)} %param.29, f32[16,1024]{1,0:T(8,128)S(1)} %div.62, f32[16,1024]{1,0:T(8,128)S(1)} %collective-permute-done.13, f32[16,1024]{1,0:T(8,128)S(1)} %mul.400, f32[16,1024]{1,0:T(8,128)S(1)} %mul.397, ...), kind=kOutput, calls=%fused_computation.21 | convolution fusion | flops 33669120 | bytes 2523140 | tf_op jit(solution)/shard_map/dot_general | solution.py:211
  (162 shorter events, 25.7 us)
Async XLA Ops:
  7.2 130.7 %copy-start = (bf16[1024,1024]{1,0:T(8,128)(2,1)S(1)}, bf16[1024,1024]{1,0:T(8,128)(2,1)}, u32[]{:S(2)}) copy-start(bf16[1024,1024]{1,0:T(8,128)(2,1)} %param.28) | copy-start | bytes 6291460
  7.2 71.2 %reduce-scatter.2.cloned.1.call-start = ((), (), s32[]{:S(2)}) async-start(), calls=%async_computation.1 | async-start | bytes 589824 | tf_op jit(solution)/shard_map/reduce_scatter | solution.py:116
  7.2 5.7 %copy-start.8 = (bf16[1024]{0:T(1024)(128)(2,1)S(1)}, bf16[1024]{0:T(1024)(128)(2,1)}, u32[]{:S(2)}) copy-start(bf16[1024]{0:T(1024)(128)(2,1)} %param.20) | copy-start | bytes 6148
  7.3 73.0 %copy-start.5 = (bf16[1024,256]{1,0:T(8,128)(2,1)S(1)}, bf16[1024,256]{1,0:T(8,128)(2,1)}, u32[]{:S(2)}) copy-start(bf16[1024,256]{1,0:T(8,128)(2,1)} %param.21) | copy-start | bytes 1572868
  7.3 73.2 %copy-start.3 = (bf16[1024,256]{1,0:T(8,128)(2,1)S(1)}, bf16[1024,256]{1,0:T(8,128)(2,1)}, u32[]{:S(2)}) copy-start(bf16[1024,256]{1,0:T(8,128)(2,1)} %param.22) | copy-start | bytes 1572868
  7.3 74.8 %copy-start.10 = (s32[128]{0:T(128)S(1)}, s32[128]{0:T(128)}, u32[]{:S(2)}) copy-start(s32[128]{0:T(128)} %param.18) | copy-start | bytes 1540
  12.9 124.0 %all-reduce.2.cloned.1.call-start = ((), (), s32[]{:S(2)}) async-start(), calls=%async_computation.2 | async-start | bytes 131072 | tf_op jit(solution)/shard_map/psum | solution.py:176
  80.7 8.6 %copy-start.6 = (bf16[16,256]{1,0:T(8,128)(2,1)}, bf16[16,256]{1,0:T(8,128)(2,1)S(1)}, u32[]{:S(2)}) copy-start(bf16[16,256]{1,0:T(8,128)(2,1)S(1)} %get-tuple-element.230) | copy-start | bytes 24580
  80.7 5.5 %collective-permute-start = (bf16[2,16,256]{2,1,0:T(8,128)(2,1)S(1)}, bf16[2,16,256]{2,1,0:T(8,128)(2,1)S(1)}, u32[]{:S(2)}, u32[]{:S(2)}) collective-permute-start(bf16[2,16,256]{2,1,0:T(8,128)(2,1)S(1)} %pad_maximum_fusion), channel_id=1, source_target_pairs={{0,4},{4,0},{8,12},{12,8},{16,20},{20,16},{24,28},{28,24},{1,5},{5... | collective-permute-start | bytes 49160 | tf_op jit(solution)/shard_map/ppermute | solution.py:15
  86.2 21.1 %copy-start.9 = (bf16[1024]{0:T(1024)(128)(2,1)S(1)}, bf16[1024]{0:T(1024)(128)(2,1)}, u32[]{:S(2)}) copy-start(bf16[1024]{0:T(1024)(128)(2,1)} %param.27) | copy-start | bytes 6148
  86.2 50.7 %copy-start.2 = (f32[16,1024]{1,0:T(8,128)S(1)}, f32[16,1024]{1,0:T(8,128)}, u32[]{:S(2)}) copy-start(f32[16,1024]{1,0:T(8,128)} %reduce-scatter.2.cloned.1.call-done) | copy-start | bytes 196612
  86.2 4.0 %collective-permute-start.1 = (bf16[2,32,256]{2,1,0:T(8,128)(2,1)S(1)}, bf16[2,32,256]{2,1,0:T(8,128)(2,1)S(1)}, u32[]{:S(2)}, u32[]{:S(2)}) collective-permute-start(bf16[2,32,256]{2,1,0:T(8,128)(2,1)S(1)} %maximum_select_fusion.3), channel_id=1, source_target_pairs={{0,8},{4,12},{8,0},{12,4},{16,24},{20,28},{24,16},{28,20},{1,9},{5... | collective-permute-start | bytes 98312 | tf_op jit(solution)/shard_map/ppermute | solution.py:15
  89.0 49.3 %copy-start.7 = (bf16[16,256]{1,0:T(8,128)(2,1)}, bf16[16,256]{1,0:T(8,128)(2,1)S(1)}, u32[]{:S(2)}) copy-start(bf16[16,256]{1,0:T(8,128)(2,1)S(1)} %convolution_convert_fusion.1) | copy-start | bytes 24580
  90.8 15.4 %copy-start.4 = (bf16[256,1024]{1,0:T(8,128)(2,1)S(1)}, bf16[256,1024]{1,0:T(8,128)(2,1)}, u32[]{:S(2)}) copy-start(bf16[256,1024]{1,0:T(8,128)(2,1)} %param.24) | copy-start | bytes 1572868
  94.5 3.8 %collective-permute-start.2 = (f32[32,4]{1,0:T(8,128)S(1)}, f32[32,4]{1,0:T(8,128)S(1)}, u32[]{:S(2)}, u32[]{:S(2)}) collective-permute-start(f32[32,4]{1,0:T(8,128)S(1)} %constant_dynamic-slice_fusion.11), channel_id=1, source_target_pairs={{0,8},{4,12},{8,0},{12,4},{16,24},{20,28},{24,16},{28,20},{1,9},{5... | collective-permute-start | bytes 1544 | tf_op jit(solution)/shard_map/ppermute | solution.py:15
  96.1 3.7 %collective-permute-start.6 = (f32[32,4]{1,0:T(8,128)S(1)}, f32[32,4]{1,0:T(8,128)S(1)}, u32[]{:S(2)}, u32[]{:S(2)}) collective-permute-start(f32[32,4]{1,0:T(8,128)S(1)} %constant_dynamic-slice_fusion.7), channel_id=1, source_target_pairs={{0,8},{4,12},{8,0},{12,4},{16,24},{20,28},{24,16},{28,20},{1,9},{5... | collective-permute-start | bytes 1544 | tf_op jit(solution)/shard_map/ppermute | solution.py:15
  96.5 5.8 %collective-permute-start.3 = (f32[32,256]{1,0:T(8,128)S(1)}, f32[32,256]{1,0:T(8,128)S(1)}, u32[]{:S(2)}, u32[]{:S(2)}) collective-permute-start(f32[32,256]{1,0:T(8,128)S(1)} %constant_dynamic-slice_fusion.10), channel_id=1, source_target_pairs={{0,8},{4,12},{8,0},{12,4},{16,24},{20,28},{24,16},{28,20},{1,9},{5... | collective-permute-start | bytes 98312 | tf_op jit(solution)/shard_map/ppermute | solution.py:15
  100.2 3.7 %collective-permute-start.4 = (f32[16,4]{1,0:T(8,128)S(1)}, f32[16,4]{1,0:T(8,128)S(1)}, u32[]{:S(2)}, u32[]{:S(2)}) collective-permute-start(f32[16,4]{1,0:T(8,128)S(1)} %constant_dynamic-slice_fusion.9), channel_id=1, source_target_pairs={{0,4},{4,0},{8,12},{12,8},{16,20},{20,16},{24,28},{28,24},{1,5},{5... | collective-permute-start | bytes 776 | tf_op jit(solution)/shard_map/ppermute | solution.py:15
  100.8 3.7 %collective-permute-start.7 = (f32[16,4]{1,0:T(8,128)S(1)}, f32[16,4]{1,0:T(8,128)S(1)}, u32[]{:S(2)}, u32[]{:S(2)}) collective-permute-start(f32[16,4]{1,0:T(8,128)S(1)} %constant_dynamic-slice_fusion.6), channel_id=1, source_target_pairs={{0,4},{4,0},{8,12},{12,8},{16,20},{20,16},{24,28},{28,24},{1,5},{5... | collective-permute-start | bytes 776 | tf_op jit(solution)/shard_map/ppermute | solution.py:15
  102.4 3.8 %collective-permute-start.5 = (f32[16,256]{1,0:T(8,128)S(1)}, f32[16,256]{1,0:T(8,128)S(1)}, u32[]{:S(2)}, u32[]{:S(2)}) collective-permute-start(f32[16,256]{1,0:T(8,128)S(1)} %constant_dynamic-slice_fusion.8), channel_id=1, source_target_pairs={{0,4},{4,0},{8,12},{12,8},{16,20},{20,16},{24,28},{28,24},{1,5},{5... | collective-permute-start | bytes 49160 | tf_op jit(solution)/shard_map/ppermute | solution.py:15
  107.0 72.8 %all-gather.2.cloned.1.call-start = ((), (), s32[]{:S(2)}) async-start(), calls=%async_computation.3 | async-start | bytes 1310720 | tf_op jit(solution)/shard_map/all_gather | solution.py:19
  138.3 3.9 %collective-permute-start.8 = (bf16[16,1024]{1,0:T(8,128)(2,1)S(1)}, bf16[16,1024]{1,0:T(8,128)(2,1)S(1)}, u32[]{:S(2)}, u32[]{:S(2)}) collective-permute-start(bf16[16,1024]{1,0:T(8,128)(2,1)S(1)} %convolution_convert_fusion), channel_id=1, source_target_pairs={{0,4},{4,0},{8,12},{12,8},{16,20},{20,16},{24,28},{28,24},{1,5},{5... | collective-permute-start | bytes 98312 | tf_op jit(solution)/shard_map/ppermute | solution.py:15
  142.2 14.3 %collective-permute-start.9 = (bf16[32,1024]{1,0:T(8,128)(2,1)S(1)}, bf16[32,1024]{1,0:T(8,128)(2,1)S(1)}, u32[]{:S(2)}, u32[]{:S(2)}) collective-permute-start(bf16[32,1024]{1,0:T(8,128)(2,1)S(1)} %maximum_select_fusion.2), channel_id=1, source_target_pairs={{0,8},{4,12},{8,0},{12,4},{16,24},{20,28},{24,16},{28,20},{1,9},{5... | collective-permute-start | bytes 196616 | tf_op jit(solution)/shard_map/ppermute | solution.py:15
  156.8 4.7 %copy-start.1 = (bf16[16,64,16,64]{3,2,1,0:T(8,128)(2,1)S(1)}, bf16[16,64,16,64]{3,2,1,0:T(8,128)(2,1)}, u32[]{:S(2)}) copy-start(bf16[16,64,16,64]{3,2,1,0:T(8,128)(2,1)} %reshape.166) | copy-start | bytes 6291460
  187.0 3.7 %collective-permute-start.10 = (f32[32,16]{0,1:T(8,128)S(1)}, f32[32,16]{0,1:T(8,128)S(1)}, u32[]{:S(2)}, u32[]{:S(2)}) collective-permute-start(f32[32,16]{0,1:T(8,128)S(1)} %constant_dynamic-slice_fusion.5), channel_id=1, source_target_pairs={{0,8},{4,12},{8,0},{12,4},{16,24},{20,28},{24,16},{28,20},{1,9},{5... | collective-permute-start | bytes 6152 | tf_op jit(solution)/shard_map/ppermute | solution.py:15
  188.6 3.7 %collective-permute-start.14 = (f32[32,16]{0,1:T(8,128)S(1)}, f32[32,16]{0,1:T(8,128)S(1)}, u32[]{:S(2)}, u32[]{:S(2)}) collective-permute-start(f32[32,16]{0,1:T(8,128)S(1)} %constant_dynamic-slice_fusion.1), channel_id=1, source_target_pairs={{0,8},{4,12},{8,0},{12,4},{16,24},{20,28},{24,16},{28,20},{1,9},{5... | collective-permute-start | bytes 6152 | tf_op jit(solution)/shard_map/ppermute | solution.py:15
  189.1 6.2 %collective-permute-start.11 = (f32[32,1024]{1,0:T(8,128)S(1)}, f32[32,1024]{1,0:T(8,128)S(1)}, u32[]{:S(2)}, u32[]{:S(2)}) collective-permute-start(f32[32,1024]{1,0:T(8,128)S(1)} %constant_dynamic-slice_fusion.4), channel_id=1, source_target_pairs={{0,8},{4,12},{8,0},{12,4},{16,24},{20,28},{24,16},{28,20},{1,9},{5... | collective-permute-start | bytes 393224 | tf_op jit(solution)/shard_map/ppermute | solution.py:15
  193.1 3.8 %collective-permute-start.12 = (f32[16,16]{0,1:T(8,128)S(1)}, f32[16,16]{0,1:T(8,128)S(1)}, u32[]{:S(2)}, u32[]{:S(2)}) collective-permute-start(f32[16,16]{0,1:T(8,128)S(1)} %constant_dynamic-slice_fusion.3), channel_id=1, source_target_pairs={{0,4},{4,0},{8,12},{12,8},{16,20},{20,16},{24,28},{28,24},{1,5},{5... | collective-permute-start | bytes 3080 | tf_op jit(solution)/shard_map/ppermute | solution.py:15
  194.7 3.7 %collective-permute-start.15 = (f32[16,16]{0,1:T(8,128)S(1)}, f32[16,16]{0,1:T(8,128)S(1)}, u32[]{:S(2)}, u32[]{:S(2)}) collective-permute-start(f32[16,16]{0,1:T(8,128)S(1)} %constant_dynamic-slice_fusion), channel_id=1, source_target_pairs={{0,4},{4,0},{8,12},{12,8},{16,20},{20,16},{24,28},{28,24},{1,5},{5... | collective-permute-start | bytes 3080 | tf_op jit(solution)/shard_map/ppermute | solution.py:15
  195.4 4.3 %collective-permute-start.13 = (f32[16,1024]{1,0:T(8,128)S(1)}, f32[16,1024]{1,0:T(8,128)S(1)}, u32[]{:S(2)}, u32[]{:S(2)}) collective-permute-start(f32[16,1024]{1,0:T(8,128)S(1)} %constant_dynamic-slice_fusion.2), channel_id=1, source_target_pairs={{0,4},{4,0},{8,12},{12,8},{16,20},{20,16},{24,28},{28,24},{1,5},{5... | collective-permute-start | bytes 196616 | tf_op jit(solution)/shard_map/ppermute | solution.py:15
Sparse Core Ops, SparseCore 0:
  13.0 65.3 reduce-scatter.1
  107.1 29.7 all-reduce.1
  163.8 15.9 all-gather.1
where the time goes:
time: 210 us; the launch traced here: 209 us
  waiting for transfers between devices  111 us (53%)
  local copies, waits for them, and re-layouts  26.4 us (13%)
  starting transfers between devices  19.8 us (9%)
  matrix products  19.4 us (9%)
  between operations  14.2 us (7%)
  blocking collectives  10.6 us (5%)
  other arithmetic  7.84 us (4%)
    reduce_scatter x1, waiting for transfers between devices, shards(): lax.psum_scatter(jnp.dot(onehot_table, embedding, preferred_element_type=...  65.4 us
    psum x1, waiting for transfers between devices, shards(): lax.psum(jnp.dot(self_context, output_weight, preferred_element_type=jnp....  29.6 us
    ppermute x16, starting transfers between devices, from_partner(): return lax.ppermute(value, axis, pairs)  19.5 us
    ppermute x16, waiting for transfers between devices, from_partner(): return lax.ppermute(value, axis, pairs)  11.2 us
    all_gather x2, blocking collectives, joined(): everything = jax.tree.map(lambda part: lax.all_gather(part, axis), x)  10.6 us
    reshape x1, local copies, waits for them, and re-layouts, shards(): image_values.reshape(row_count, patch_count, HEADS, head_size)  6.4 us
    reshape x1, local copies, waits for them, and re-layouts, shards(): patch_keys = image_keys.reshape(row_count, patch_count, HEADS, head_size)  6.37 us
    dot_general x1, matrix products, shards(): jnp.dot(onehot_table, embedding, preferred_element_type=jnp.float32)  5.58 us
  transfers between devices with their start and end apart: 19, of which 13 were waited for; matrix products, arithmetic and copies ran while one was open for 11% of the time, Pallas kernels for 0%

commit v1 on v0

--- a/solution.py
+++ b/solution.py
@@ -7,6 +7,12 @@
 D = 1024
 HEADS = 16
 BEAMS = 4
+
+
+def summed_here(x, name):
+    parts = lax.all_gather(x, name, axis=0, tiled=False)
+    total = parts.sum(axis=0)
+    return total
 
 
 def from_partner(value, axis, distance):
@@ -173,7 +179,7 @@
     ] * value_heads.astype(jnp.float32)
     self_context = weighted / sums[..., None]
     self_context = self_context.reshape(row_count, width_here).astype(jnp.bfloat16)
-    middle = tokens + lax.psum(
+    middle = tokens + summed_here(
         jnp.dot(self_context, output_weight, preferred_element_type=jnp.float32), "patch"
     )
     probes = jnp.dot(

time: 210 us -> 184 us (0.88)
  waiting for transfers between devices: 111 us -> 81.8 us
  blocking collectives: 10.6 us -> 16.6 us
  starting transfers between devices: 19.8 us -> 17.7 us
    psum x1 -> x0, waiting for transfers between devices: 29.6 us -> none  [shards(): lax.psum(jnp.dot(self_context, output_weight, preferred_element_type=jnp....]
    all_gather x0 -> x1, blocking collectives: none -> 5.95 us  [summed_here(): parts = lax.all_gather(x, name, axis=0, tiled=False)]
  transfers between devices with their start and end apart: 19 -> 18, of which waited for: 13 -> 12; matrix products, arithmetic and copies ran while one was open for 11% -> 12% of each run, Pallas kernels for 0% -> 0%
where the time goes in v1:
time: 184 us; the launch traced here: 183 us
  waiting for transfers between devices  81.8 us (44%)
  local copies, waits for them, and re-layouts  26.4 us (14%)
  matrix products  18.7 us (10%)
  starting transfers between devices  17.7 us (10%)
  blocking collectives  16.6 us (9%)
  between operations  14.5 us (8%)
  other arithmetic  7.02 us (4%)
    reduce_scatter x1, waiting for transfers between devices, shards(): lax.psum_scatter(jnp.dot(onehot_table, embedding, preferred_element_type=...  65.4 us
    ppermute x16, starting transfers between devices, from_partner(): return lax.ppermute(value, axis, pairs)  17.6 us
    ppermute x16, waiting for transfers between devices, from_partner(): return lax.ppermute(value, axis, pairs)  12.1 us
    all_gather x2, blocking collectives, joined(): everything = jax.tree.map(lambda part: lax.all_gather(part, axis), x)  10.6 us
    reshape x1, local copies, waits for them, and re-layouts, shards(): image_values.reshape(row_count, patch_count, HEADS, head_size)  6.41 us
    reshape x1, local copies, waits for them, and re-layouts, shards(): patch_keys = image_keys.reshape(row_count, patch_count, HEADS, head_size)  6.38 us
    all_gather x1, blocking collectives, summed_here(): parts = lax.all_gather(x, name, axis=0, tiled=False)  5.95 us
    dot_general x1, matrix products, shards(): jnp.dot(onehot_table, embedding, preferred_element_type=jnp.float32)  5.58 us
  transfers between devices with their start and end apart: 18, of which 12 were waited for; matrix products, arithmetic and copies ran while one was open for 12% of the time, Pallas kernels for 0%

profile of v1, /device:TPU:0, one launch (start us, length us, event | category | flops | bytes accessed | tf_op | source)
XLA Modules:
  0.0 182.8 jit_solution(8345179263032035695)
XLA Ops:
  7.3 5.6 %fusion.7 = f32[128,1024]{1,0:T(8,128)} fusion(bf16[4000,1024]{1,0:T(8,128)(2,1)} %param.19, s32[4000]{0:T(1024)S(1)} %iota_add_fusion, s32[128]{0:T(128)} %param.17), kind=kOutput, calls=%fused_computation.12 | convolution fusion | flops 1049088000 | bytes 8732800 | tf_op jit(solution)/shard_map/dot_general | solution.py:123
  13.0 65.4 %reduce-scatter.2.cloned.1.call-done = f32[16,1024]{1,0:T(8,128)} async-done(((f32[128,1024]{1,0:T(8,128)}), f32[16,1024]{1,0:T(8,128)}) %reduce-scatter.2.cloned.1.call-update) | async-done | bytes 65552 | tf_op jit(solution)/shard_map/reduce_scatter | solution.py:122
  80.7 1.4 collective-permute-start
  82.1 1.6 copy.108
  83.9 2.3 %copy.114 = bf16[16,128,256]{1,2,0:T(8,128)(2,1)} copy(bf16[16,128,256]{2,1,0:T(8,128)(2,1)} %param.26) | data formatting | bytes 2097152 | tf_op args[9]
  86.2 1.6 collective-permute-start.1
  87.9 1.2 convolution_convert_fusion.1
  92.0 1.9 %convolution_bitcast_fusion = f32[4,16,4,64]{3,0,2,1:T(4,128)S(1)} fusion(bf16[16,128,4,64]{1,3,2,0:T(8,128)(2,1)} %bitcast.83, f32[4,16,4,128]{3,0,2,1:T(4,128)S(1)} %get-tuple-element.228, f32[4,16]{0,1:T(8,128)S(1)} %copy.113, f32[4,16,4]{0,2,1:T(4,128)S(1)} %copy.112), kind=kOutput, calls=%fused_computation.17 | convolution fusion | flops 4292608 | bytes 1246464 | tf_op jit(solution)/shard_map/bihl,ilhe->bihe/dot_general | solution.py:164
  94.5 1.6 collective-permute-start.2
  96.6 1.5 collective-permute-start.3
  98.3 1.6 collective-permute-done.6
  100.9 1.5 collective-permute-start.7
  106.4 5.9 %all-gather = f32[64,1024]{1,0:T(8,128)S(1)} all-gather(f32[16,1024]{1,0:T(8,128)S(1)} %fusion.41), channel_id=2, replica_groups=mesh['dp'=8,'patch'=4] {'patch'}, dimensions={0}, use_global_device_ids=true | all-gather | bytes 327680 | tf_op jit(solution)/shard_map/all_gather | solution.py:13
  113.5 3.4 %collective-permute-done.8 = bf16[16,1024]{1,0:T(8,128)(2,1)S(1)} collective-permute-done((bf16[16,1024]{1,0:T(8,128)(2,1)S(1)}, bf16[16,1024]{1,0:T(8,128)(2,1)S(1)}, u32[]{:S(2)}, u32[]{:S(2)}) %collective-permute-start.8) | collective-permute-done | bytes 32800 | tf_op jit(solution)/shard_map/ppermute | solution.py:21
  117.5 6.4 %reshape.165 = bf16[16,64,16,64]{3,2,1,0:T(8,128)(2,1)} reshape(bf16[1,16,64,1024]{3,2,1,0:T(8,128)(2,1)} %param.30) | data formatting | bytes 4194304 | tf_op jit(solution)/shard_map/reshape | solution.py:190
  123.8 6.4 %reshape.166 = bf16[16,64,16,64]{3,2,1,0:T(8,128)(2,1)} reshape(bf16[1,16,64,1024]{3,2,1,0:T(8,128)(2,1)} %param.31) | data formatting | bytes 4194304 | tf_op jit(solution)/shard_map/reshape | solution.py:191
  130.5 4.7 %fusion.51 = (f32[4,16,16]{0,2,1:T(8,128)S(1)}, f32[4,16,16,64]{3,0,2,1:T(4,128)S(1)}) fusion(bf16[16,64,16,64]{3,2,1,0:T(8,128)(2,1)} %reshape.165, bf16[4,16,16,64]{3,2,1,0:T(8,128)(2,1)S(1)} %select_n.148), kind=kOutput, calls=%fused_computation.109 | convolution fusion | flops 8518656 | bytes 2494464 | tf_op jit(solution)/shard_map/bihe,iphe->bihp/dot_general | solution.py:193
  135.2 1.3 fusion.9
  138.6 5.2 %all_gather.18 = f32[4,64,16]{1,2,0:T(8,128)S(1)} all-gather(f32[1,64,16]{1,2,0:T(8,128)S(1)} %all_gather_reshape.10), channel_id=1, replica_groups=mesh['dp'=8,'patch'=4] {'patch'}, dimensions={0}, use_global_device_ids=true | all-gather | bytes 20480 | tf_op jit(solution)/shard_map/all_gather | solution.py:25
  143.8 5.4 %all_gather.17 = f32[4,64,16]{1,2,0:T(8,128)S(1)} all-gather(f32[1,64,16]{1,2,0:T(8,128)S(1)} %all_gather_reshape.9), channel_id=1, replica_groups=mesh['dp'=8,'patch'=4] {'patch'}, dimensions={0}, use_global_device_ids=true | all-gather | bytes 20480 | tf_op jit(solution)/shard_map/all_gather | solution.py:25
  149.2 4.3 %all-gather.3.cloned.1.call-done = f32[4,64,1024]{2,1,0:T(8,128)} async-done(((f32[1,64,1024]{2,1,0:T(8,128)}), f32[4,64,1024]{2,1,0:T(8,128)}) %all-gather.3.cloned.1.call-update) | async-done | bytes 1048592 | tf_op jit(solution)/shard_map/all_gather | solution.py:25
  154.5 6.1 %while.19 = (s32[]{:T(128)}, f32[64,16]{0,1:T(8,128)S(1)}, f32[64,16]{0,1:T(8,128)S(1)}, f32[64,1024]{1,0:T(8,128)S(1)}, f32[4,64,16]{1,2,0:T(8,128)S(1)}, /*ind...) while((s32[]{:T(128)}, f32[64,16]{0,1:T(8,128)S(1)}, ...), condition=%wide.region_11.12_spmd, body=%wide.region_10.11_spmd.sunk | while | flops 202757 | bytes 2941079 | solution.py:31
  155.4 1.1 fusion.67
  157.5 1.1 fusion.67
  159.5 1.1 fusion.67
  160.7 1.5 collective-permute-start.10
  162.8 1.6 collective-permute-start.11
  164.4 1.6 collective-permute-done.14
  166.8 1.5 collective-permute-start.12
  169.0 1.5 collective-permute-start.13
  170.6 1.5 collective-permute-done.15
  173.4 2.6 %fusion.19 = bf16[16,1024]{1,0:T(8,128)(2,1)} fusion(f32[16,1024]{1,0:T(8,128)S(1)} %get-tuple-element.210, bf16[1024,1024]{1,0:T(8,128)(2,1)} %param.29, f32[16,1024]{1,0:T(8,128)S(1)} %div.62, f32[16,1024]{1,0:T(8,128)S(1)} %collective-permute-done.13, f32[16,1024]{1,0:T(8,128)S(1)} %mul.400, f32[16,1024]{1,0:T(8,128)S(1)} %mul.397, ...), kind=kOutput, calls=%fused_computation.21 | convolution fusion | flops 33669120 | bytes 2523140 | tf_op jit(solution)/shard_map/dot_general | solution.py:217
  (161 shorter events, 23.0 us)
Async XLA Ops:
  7.2 105.3 %copy-start = (bf16[1024,1024]{1,0:T(8,128)(2,1)S(1)}, bf16[1024,1024]{1,0:T(8,128)(2,1)}, u32[]{:S(2)}) copy-start(bf16[1024,1024]{1,0:T(8,128)(2,1)} %param.28) | copy-start | bytes 6291460
  7.2 71.2 %reduce-scatter.2.cloned.1.call-start = ((), (), s32[]{:S(2)}) async-start(), calls=%async_computation.1 | async-start | bytes 589824 | tf_op jit(solution)/shard_map/reduce_scatter | solution.py:122
  7.2 5.7 %copy-start.8 = (bf16[1024]{0:T(1024)(128)(2,1)S(1)}, bf16[1024]{0:T(1024)(128)(2,1)}, u32[]{:S(2)}) copy-start(bf16[1024]{0:T(1024)(128)(2,1)} %param.20) | copy-start | bytes 6148
  7.3 73.0 %copy-start.5 = (bf16[1024,256]{1,0:T(8,128)(2,1)S(1)}, bf16[1024,256]{1,0:T(8,128)(2,1)}, u32[]{:S(2)}) copy-start(bf16[1024,256]{1,0:T(8,128)(2,1)} %param.21) | copy-start | bytes 1572868
  7.3 73.2 %copy-start.3 = (bf16[1024,256]{1,0:T(8,128)(2,1)S(1)}, bf16[1024,256]{1,0:T(8,128)(2,1)}, u32[]{:S(2)}) copy-start(bf16[1024,256]{1,0:T(8,128)(2,1)} %param.22) | copy-start | bytes 1572868
  7.3 74.8 %copy-start.10 = (s32[128]{0:T(128)S(1)}, s32[128]{0:T(128)}, u32[]{:S(2)}) copy-start(s32[128]{0:T(128)} %param.18) | copy-start | bytes 1540
  12.9 73.3 %copy-start.9 = (bf16[1024]{0:T(1024)(128)(2,1)S(1)}, bf16[1024]{0:T(1024)(128)(2,1)}, u32[]{:S(2)}) copy-start(bf16[1024]{0:T(1024)(128)(2,1)} %param.27) | copy-start | bytes 6148
  12.9 140.6 %all-gather.3.cloned.1.call-start = ((), (), s32[]{:S(2)}) async-start(), calls=%async_computation.2 | async-start | bytes 1310720 | tf_op jit(solution)/shard_map/all_gather | solution.py:25
  80.7 8.6 %copy-start.6 = (bf16[16,256]{1,0:T(8,128)(2,1)}, bf16[16,256]{1,0:T(8,128)(2,1)S(1)}, u32[]{:S(2)}) copy-start(bf16[16,256]{1,0:T(8,128)(2,1)S(1)} %get-tuple-element.230) | copy-start | bytes 24580
  80.7 5.5 %collective-permute-start = (bf16[2,16,256]{2,1,0:T(8,128)(2,1)S(1)}, bf16[2,16,256]{2,1,0:T(8,128)(2,1)S(1)}, u32[]{:S(2)}, u32[]{:S(2)}) collective-permute-start(bf16[2,16,256]{2,1,0:T(8,128)(2,1)S(1)} %pad_maximum_fusion), channel_id=1, source_target_pairs={{0,4},{4,0},{8,12},{12,8},{16,20},{20,16},{24,28},{28,24},{1,5},{5... | collective-permute-start | bytes 49160 | tf_op jit(solution)/shard_map/ppermute | solution.py:21
  86.2 26.2 %copy-start.2 = (f32[16,1024]{1,0:T(8,128)S(1)}, f32[16,1024]{1,0:T(8,128)}, u32[]{:S(2)}) copy-start(f32[16,1024]{1,0:T(8,128)} %reduce-scatter.2.cloned.1.call-done) | copy-start | bytes 196612
  86.2 4.0 %collective-permute-start.1 = (bf16[2,32,256]{2,1,0:T(8,128)(2,1)S(1)}, bf16[2,32,256]{2,1,0:T(8,128)(2,1)S(1)}, u32[]{:S(2)}, u32[]{:S(2)}) collective-permute-start(bf16[2,32,256]{2,1,0:T(8,128)(2,1)S(1)} %maximum_select_fusion.3), channel_id=1, source_target_pairs={{0,8},{4,12},{8,0},{12,4},{16,24},{20,28},{24,16},{28,20},{1,9},{5... | collective-permute-start | bytes 98312 | tf_op jit(solution)/shard_map/ppermute | solution.py:21
  89.1 23.9 %copy-start.7 = (bf16[16,256]{1,0:T(8,128)(2,1)}, bf16[16,256]{1,0:T(8,128)(2,1)S(1)}, u32[]{:S(2)}) copy-start(bf16[16,256]{1,0:T(8,128)(2,1)S(1)} %convolution_convert_fusion.1) | copy-start | bytes 24580
  90.8 15.4 %copy-start.4 = (bf16[256,1024]{1,0:T(8,128)(2,1)S(1)}, bf16[256,1024]{1,0:T(8,128)(2,1)}, u32[]{:S(2)}) copy-start(bf16[256,1024]{1,0:T(8,128)(2,1)} %param.24) | copy-start | bytes 1572868
  94.5 3.8 %collective-permute-start.2 = (f32[32,4]{1,0:T(8,128)S(1)}, f32[32,4]{1,0:T(8,128)S(1)}, u32[]{:S(2)}, u32[]{:S(2)}) collective-permute-start(f32[32,4]{1,0:T(8,128)S(1)} %constant_dynamic-slice_fusion.11), channel_id=1, source_target_pairs={{0,8},{4,12},{8,0},{12,4},{16,24},{20,28},{24,16},{28,20},{1,9},{5... | collective-permute-start | bytes 1544 | tf_op jit(solution)/shard_map/ppermute | solution.py:21
  96.1 3.7 %collective-permute-start.6 = (f32[32,4]{1,0:T(8,128)S(1)}, f32[32,4]{1,0:T(8,128)S(1)}, u32[]{:S(2)}, u32[]{:S(2)}) collective-permute-start(f32[32,4]{1,0:T(8,128)S(1)} %constant_dynamic-slice_fusion.7), channel_id=1, source_target_pairs={{0,8},{4,12},{8,0},{12,4},{16,24},{20,28},{24,16},{28,20},{1,9},{5... | collective-permute-start | bytes 1544 | tf_op jit(solution)/shard_map/ppermute | solution.py:21
  96.6 5.8 %collective-permute-start.3 = (f32[32,256]{1,0:T(8,128)S(1)}, f32[32,256]{1,0:T(8,128)S(1)}, u32[]{:S(2)}, u32[]{:S(2)}) collective-permute-start(f32[32,256]{1,0:T(8,128)S(1)} %constant_dynamic-slice_fusion.10), channel_id=1, source_target_pairs={{0,8},{4,12},{8,0},{12,4},{16,24},{20,28},{24,16},{28,20},{1,9},{5... | collective-permute-start | bytes 98312 | tf_op jit(solution)/shard_map/ppermute | solution.py:21
  100.3 3.7 %collective-permute-start.4 = (f32[16,4]{1,0:T(8,128)S(1)}, f32[16,4]{1,0:T(8,128)S(1)}, u32[]{:S(2)}, u32[]{:S(2)}) collective-permute-start(f32[16,4]{1,0:T(8,128)S(1)} %constant_dynamic-slice_fusion.9), channel_id=1, source_target_pairs={{0,4},{4,0},{8,12},{12,8},{16,20},{20,16},{24,28},{28,24},{1,5},{5... | collective-permute-start | bytes 776 | tf_op jit(solution)/shard_map/ppermute | solution.py:21
  100.9 3.7 %collective-permute-start.7 = (f32[16,4]{1,0:T(8,128)S(1)}, f32[16,4]{1,0:T(8,128)S(1)}, u32[]{:S(2)}, u32[]{:S(2)}) collective-permute-start(f32[16,4]{1,0:T(8,128)S(1)} %constant_dynamic-slice_fusion.6), channel_id=1, source_target_pairs={{0,4},{4,0},{8,12},{12,8},{16,20},{20,16},{24,28},{28,24},{1,5},{5... | collective-permute-start | bytes 776 | tf_op jit(solution)/shard_map/ppermute | solution.py:21
  102.4 3.8 %collective-permute-start.5 = (f32[16,256]{1,0:T(8,128)S(1)}, f32[16,256]{1,0:T(8,128)S(1)}, u32[]{:S(2)}, u32[]{:S(2)}) collective-permute-start(f32[16,256]{1,0:T(8,128)S(1)} %constant_dynamic-slice_fusion.8), channel_id=1, source_target_pairs={{0,4},{4,0},{8,12},{12,8},{16,20},{20,16},{24,28},{28,24},{1,5},{5... | collective-permute-start | bytes 49160 | tf_op jit(solution)/shard_map/ppermute | solution.py:21
  112.9 3.9 %collective-permute-start.8 = (bf16[16,1024]{1,0:T(8,128)(2,1)S(1)}, bf16[16,1024]{1,0:T(8,128)(2,1)S(1)}, u32[]{:S(2)}, u32[]{:S(2)}) collective-permute-start(bf16[16,1024]{1,0:T(8,128)(2,1)S(1)} %convolution_convert_fusion), channel_id=1, source_target_pairs={{0,4},{4,0},{8,12},{12,8},{16,20},{20,16},{24,28},{28,24},{1,5},{5... | collective-permute-start | bytes 98312 | tf_op jit(solution)/shard_map/ppermute | solution.py:21
  116.9 13.4 %collective-permute-start.9 = (bf16[32,1024]{1,0:T(8,128)(2,1)S(1)}, bf16[32,1024]{1,0:T(8,128)(2,1)S(1)}, u32[]{:S(2)}, u32[]{:S(2)}) collective-permute-start(bf16[32,1024]{1,0:T(8,128)(2,1)S(1)} %maximum_select_fusion.2), channel_id=1, source_target_pairs={{0,8},{4,12},{8,0},{12,4},{16,24},{20,28},{24,16},{28,20},{1,9},{5... | collective-permute-start | bytes 196616 | tf_op jit(solution)/shard_map/ppermute | solution.py:21
  130.5 4.7 %copy-start.1 = (bf16[16,64,16,64]{3,2,1,0:T(8,128)(2,1)S(1)}, bf16[16,64,16,64]{3,2,1,0:T(8,128)(2,1)}, u32[]{:S(2)}) copy-start(bf16[16,64,16,64]{3,2,1,0:T(8,128)(2,1)} %reshape.166) | copy-start | bytes 6291460
  160.7 3.7 %collective-permute-start.10 = (f32[32,16]{0,1:T(8,128)S(1)}, f32[32,16]{0,1:T(8,128)S(1)}, u32[]{:S(2)}, u32[]{:S(2)}) collective-permute-start(f32[32,16]{0,1:T(8,128)S(1)} %constant_dynamic-slice_fusion.5), channel_id=1, source_target_pairs={{0,8},{4,12},{8,0},{12,4},{16,24},{20,28},{24,16},{28,20},{1,9},{5... | collective-permute-start | bytes 6152 | tf_op jit(solution)/shard_map/ppermute | solution.py:21
  162.2 3.7 %collective-permute-start.14 = (f32[32,16]{0,1:T(8,128)S(1)}, f32[32,16]{0,1:T(8,128)S(1)}, u32[]{:S(2)}, u32[]{:S(2)}) collective-permute-start(f32[32,16]{0,1:T(8,128)S(1)} %constant_dynamic-slice_fusion.1), channel_id=1, source_target_pairs={{0,8},{4,12},{8,0},{12,4},{16,24},{20,28},{24,16},{28,20},{1,9},{5... | collective-permute-start | bytes 6152 | tf_op jit(solution)/shard_map/ppermute | solution.py:21
  162.8 6.2 %collective-permute-start.11 = (f32[32,1024]{1,0:T(8,128)S(1)}, f32[32,1024]{1,0:T(8,128)S(1)}, u32[]{:S(2)}, u32[]{:S(2)}) collective-permute-start(f32[32,1024]{1,0:T(8,128)S(1)} %constant_dynamic-slice_fusion.4), channel_id=1, source_target_pairs={{0,8},{4,12},{8,0},{12,4},{16,24},{20,28},{24,16},{28,20},{1,9},{5... | collective-permute-start | bytes 393224 | tf_op jit(solution)/shard_map/ppermute | solution.py:21
  166.8 3.8 %collective-permute-start.12 = (f32[16,16]{0,1:T(8,128)S(1)}, f32[16,16]{0,1:T(8,128)S(1)}, u32[]{:S(2)}, u32[]{:S(2)}) collective-permute-start(f32[16,16]{0,1:T(8,128)S(1)} %constant_dynamic-slice_fusion.3), channel_id=1, source_target_pairs={{0,4},{4,0},{8,12},{12,8},{16,20},{20,16},{24,28},{28,24},{1,5},{5... | collective-permute-start | bytes 3080 | tf_op jit(solution)/shard_map/ppermute | solution.py:21
  168.4 3.7 %collective-permute-start.15 = (f32[16,16]{0,1:T(8,128)S(1)}, f32[16,16]{0,1:T(8,128)S(1)}, u32[]{:S(2)}, u32[]{:S(2)}) collective-permute-start(f32[16,16]{0,1:T(8,128)S(1)} %constant_dynamic-slice_fusion), channel_id=1, source_target_pairs={{0,4},{4,0},{8,12},{12,8},{16,20},{20,16},{24,28},{28,24},{1,5},{5... | collective-permute-start | bytes 3080 | tf_op jit(solution)/shard_map/ppermute | solution.py:21
  169.0 4.3 %collective-permute-start.13 = (f32[16,1024]{1,0:T(8,128)S(1)}, f32[16,1024]{1,0:T(8,128)S(1)}, u32[]{:S(2)}, u32[]{:S(2)}) collective-permute-start(f32[16,1024]{1,0:T(8,128)S(1)} %constant_dynamic-slice_fusion.2), channel_id=1, source_target_pairs={{0,4},{4,0},{8,12},{12,8},{16,20},{20,16},{24,28},{28,24},{1,5},{5... | collective-permute-start | bytes 196616 | tf_op jit(solution)/shard_map/ppermute | solution.py:21
Sparse Core Ops, SparseCore 0:
  13.0 65.3 reduce-scatter.1
  137.5 15.9 all-gather.2
